TPU v7x, 32 devices: a whole 2x2x4 slice. The times are simulated.
32 devices in a mesh: dp: 2 (over x), row: 4 (over z), col: 4 (over y, core).
Axes of the slice: x: 2, y: 2, z: 4, core: 2. Of those that a mesh axis runs over, the one named last changes fastest.
Arguments:
- expand_gradient: bfloat16 [2, 4096, 5120], P('dp', 'row', 'col'), may hold values from -24 to 24, as said below
- expand_master: float32 [4096, 5120], P(('row', 'dp'), 'col'), may hold values from -0.12 to 0.12
- expand_rows: float32 [4096], P(('row', 'dp')), may hold values from 0.01 to 1
- expand_columns: float32 [5120], P('col'), may hold values from 0.01 to 1
- contract_gradient: bfloat16 [2, 5120, 4096], P('dp', 'row', 'col'), may hold values from -24 to 24, as said below
- contract_master: float32 [5120, 4096], P(('row', 'dp'), 'col'), may hold values from -0.12 to 0.12
- contract_rows: float32 [5120], P(('row', 'dp')), may hold values from 0.01 to 1
- contract_columns: float32 [4096], P('col'), may hold values from 0.01 to 1
- attend_gradient: bfloat16 [2, 4096, 4096], P('dp', 'row', 'col'), may hold values from -24 to 24, as said below
- attend_master: float32 [4096, 4096], P(('row', 'dp'), 'col'), may hold values from -0.12 to 0.12
- attend_rows: float32 [4096], P(('row', 'dp')), may hold values from 0.01 to 1
- attend_columns: float32 [4096], P('col'), may hold values from 0.01 to 1
Outputs:
- expand_updated: float32 [4096, 5120], P(('row', 'dp'), 'col')
- expand_weights: bfloat16 [4096, 5120], P('row', 'col')
- expand_rows_next: float32 [4096], P(('row', 'dp'))
- expand_columns_next: float32 [5120], P('col')
- expand_step: float32 [4096, 5120], P(('row', 'dp'), 'col')
- contract_updated: float32 [5120, 4096], P(('row', 'dp'), 'col')
- contract_weights: bfloat16 [5120, 4096], P('row', 'col')
- contract_rows_next: float32 [5120], P(('row', 'dp'))
- contract_columns_next: float32 [4096], P('col')
- contract_step: float32 [5120, 4096], P(('row', 'dp'), 'col')
- attend_updated: float32 [4096, 4096], P(('row', 'dp'), 'col')
- attend_weights: bfloat16 [4096, 4096], P('row', 'col')
- attend_rows_next: float32 [4096], P(('row', 'dp'))
- attend_columns_next: float32 [4096], P('col')
- attend_step: float32 [4096, 4096], P(('row', 'dp'), 'col')
Inputs may be any that keep to these rules, and one draw needn't show every extreme that they name: `expand_gradient`: each replica's gradient, of any scale from entry to entry. `contract_gradient`: each replica's gradient, of any scale from entry to entry. `attend_gradient`: each replica's gradient, of any scale from entry to entry.
All inputs are finite; a program needn't handle non-finite values.
Results may differ from a plain program's by a relative error of at most 0.0004.
Values may be sent and summed in bfloat16 or wider, within the bound.
A program may use at most 128 MiB of HBM per device.

v0:
```python
import jax
import jax.numpy as jnp
from jax import lax
from jax.sharding import PartitionSpec as P

tiny_square = 1e-30
decay_rate = 0.9
learn_rate = 0.01


def finish(update_raw, clip_total, master, full_size):
    clip_scale = jnp.maximum(1.0, jnp.sqrt(clip_total / full_size))
    step_taken = update_raw / clip_scale
    updated = master - learn_rate * step_taken
    weights = lax.all_gather(updated.astype(jnp.bfloat16), "dp", axis=0, tiled=True)
    return (updated, weights, step_taken)


def reduce_gradient(gradient, dp_count):
    received = lax.all_to_all(gradient, "dp", split_axis=1, concat_axis=0, tiled=True)
    summed = jnp.sum(received.astype(jnp.float32), axis=0)
    return summed / dp_count


def body(
    expand_gradient,
    expand_master,
    expand_rows,
    expand_columns,
    contract_gradient,
    contract_master,
    contract_rows,
    contract_columns,
    attend_gradient,
    attend_master,
    attend_rows,
    attend_columns,
):
    groups = (
        (expand_gradient, expand_master, expand_rows, expand_columns),
        (contract_gradient, contract_master, contract_rows, contract_columns),
        (attend_gradient, attend_master, attend_rows, attend_columns),
    )
    dp_count = lax.axis_size("dp")
    col_count = lax.axis_size("col")
    split_count = dp_count * lax.axis_size("row")
    means = []
    for gradient, master, row_stat, column_stat in groups:
        means.append(reduce_gradient(gradient, dp_count))
    squares = [mean_grad * mean_grad + tiny_square for mean_grad in means]
    row_parts = [jnp.sum(square_block, axis=1) for square_block in squares]
    column_parts = [jnp.sum(square_block, axis=0) for square_block in squares]
    heights = [mean_grad.shape[0] * split_count for mean_grad in means]
    widths = [mean_grad.shape[1] * col_count for mean_grad in means]
    outputs = []
    for which in range(3):
        row_total = lax.psum(row_parts[which], "col")
        rows_next = decay_rate * groups[which][2] + (1.0 - decay_rate) * row_total / widths[which]
        column_total, rows_sum = lax.psum((column_parts[which], jnp.sum(rows_next)), ("dp", "row"))
        columns_next = (
            decay_rate * groups[which][3] + (1.0 - decay_rate) * column_total / heights[which]
        )
        row_mean = rows_sum / heights[which]
        update_raw = means[which] * jnp.sqrt(
            row_mean / (rows_next[:, None] * columns_next[None, :])
        )
        clip_total = lax.psum(jnp.sum(update_raw * update_raw), ("dp", "row", "col"))
        updated, weights, step_taken = finish(
            update_raw, clip_total, groups[which][1], heights[which] * widths[which]
        )
        outputs.extend([updated, weights, rows_next, columns_next, step_taken])
    return tuple(outputs)


def solution(mesh):
    return jax.shard_map(
        body,
        mesh=mesh,
        in_specs=(
            P("dp", "row", "col"),
            P(("row", "dp"), "col"),
            P(("row", "dp")),
            P("col"),
            P("dp", "row", "col"),
            P(("row", "dp"), "col"),
            P(("row", "dp")),
            P("col"),
            P("dp", "row", "col"),
            P(("row", "dp"), "col"),
            P(("row", "dp")),
            P("col"),
        ),
        out_specs=(
            P(("row", "dp"), "col"),
            P("row", "col"),
            P(("row", "dp")),
            P("col"),
            P(("row", "dp"), "col"),
            P(("row", "dp"), "col"),
            P("row", "col"),
            P(("row", "dp")),
            P("col"),
            P(("row", "dp"), "col"),
            P(("row", "dp"), "col"),
            P("row", "col"),
            P(("row", "dp")),
            P("col"),
            P(("row", "dp"), "col"),
        ),
        check_vma=False,
    )
```

profile of v0, /device:TPU:0, one launch (start us, length us, event | category | flops | bytes accessed | tf_op | source)
XLA Modules:
  0.0 387.2 jit_solution(6910142270513207531)
XLA Ops:
  7.2 6.8 %copy.41 = bf16[1,1024,1024]{2,0,1:T(2,128)(2,1)} copy(bf16[1,1024,1024]{2,1,0:T(8,128)(2,1)} %param.20) | data formatting | bytes 4194304 | tf_op args[8]
  13.9 0.5 broadcast.37
  14.4 12.8 %reduce.2 = bf16[1024,1024]{1,0:T(8,128)(2,1)S(1)} reduce(bf16[1024,1,1024]{2,1,0:T(2,128)(2,1)} %bitcast.22, bf16[]{:T(256)} %broadcast.37), dimensions={1}, to_apply=%bitcast.17.reduce_sub_computation | reduce | bytes 4194306
  27.2 2.5 reshape.58
  29.7 5.5 %all-to-all-start.2 = ((bf16[2,2,262144]{2,1,0:T(2,128)(2,1)}), bf16[2,2,262144]{2,1,0:T(2,128)(2,1)}, u32[]{:S(2)}, u32[]{:S(2)}) async-start(bf16[2,2,262144]{2,1,0:T(2,128)(2,1)} %reshape.58), calls=%async_computation.2 | async-start | bytes 4194304 | tf_op jit(solution)/shard_map/all_to_all | solution.py:20
  35.2 6.4 %copy.40 = bf16[1,1024,1280]{2,0,1:T(2,128)(2,1)} copy(bf16[1,1024,1280]{2,1,0:T(8,128)(2,1)S(1)} %copy-done.4) | data formatting | bytes 5242880 | tf_op args[0]
  41.6 26.6 %reduce = bf16[1024,1280]{1,0:T(8,128)(2,1)S(1)} reduce(bf16[1024,1,1280]{2,1,0:T(2,128)(2,1)} %bitcast.21, bf16[]{:T(256)} %broadcast.37), dimensions={1}, to_apply=%bitcast.16.reduce_sub_computation | reduce | bytes 5242882
  68.2 1.8 reshape.54
  70.0 5.8 %all-to-all-start = ((bf16[2,2,327680]{2,1,0:T(2,128)(2,1)}), bf16[2,2,327680]{2,1,0:T(2,128)(2,1)}, u32[]{:S(2)}, u32[]{:S(2)}) async-start(bf16[2,2,327680]{2,1,0:T(2,128)(2,1)} %reshape.54), calls=%async_computation | async-start | bytes 5242880 | tf_op jit(solution)/shard_map/all_to_all | solution.py:20
  75.9 18.2 %copy.39 = bf16[1,1280,1024]{2,0,1:T(2,128)(2,1)} copy(bf16[1,1280,1024]{2,1,0:T(8,128)(2,1)S(1)} %copy-done.5) | data formatting | bytes 5242880 | tf_op args[4]
  94.1 15.6 %reduce.1 = bf16[1280,1024]{1,0:T(8,128)(2,1)S(1)} reduce(bf16[1280,1,1024]{2,1,0:T(2,128)(2,1)} %bitcast.18, bf16[]{:T(256)} %broadcast.37), dimensions={1}, to_apply=%bitcast.15.reduce_sub_computation | reduce | bytes 5242882
  109.6 3.0 reshape.56
  112.6 4.1 %all-to-all-start.1 = ((bf16[2,2,327680]{2,1,0:T(2,128)(2,1)}), bf16[2,2,327680]{2,1,0:T(2,128)(2,1)S(1)}, u32[]{:S(2)}, u32[]{:S(2)}) async-start(bf16[2,2,327680]{2,1,0:T(2,128)(2,1)} %reshape.56), calls=%async_computation.1 | async-start | bytes 5242880 | tf_op jit(solution)/shard_map/all_to_all | solution.py:20
  116.8 0.2 all-gather.8.cloned.1.call-start
  116.9 4.3 %reshape.59 = bf16[1024,1,1024]{2,1,0:T(2,128)(2,1)} reshape(bf16[2,2,262144]{2,1,0:T(2,128)(2,1)} %all-to-all-done.2) | data formatting | bytes 4194304
  121.2 3.0 copy.35
  124.2 0.4 convert_reduce_fusion.2
  124.7 0.0 copy-start.1
  124.7 1.3 copy-done.1
  126.0 0.5 fusion.5
  126.5 5.1 %reshape.55 = bf16[1024,1,1280]{2,1,0:T(2,128)(2,1)} reshape(bf16[2,2,327680]{2,1,0:T(2,128)(2,1)} %all-to-all-done) | data formatting | bytes 5242880
  131.5 2.9 copy.31
  134.4 0.5 convert_reduce_fusion.1
  134.9 0.0 copy-start
  134.9 1.5 copy-done
  136.4 0.6 fusion.1
  137.0 11.3 %all-to-all-done.1 = bf16[2,2,327680]{2,1,0:T(2,128)(2,1)S(1)} async-done(((bf16[2,2,327680]{2,1,0:T(2,128)(2,1)}), bf16[2,2,327680]{2,1,0:T(2,128)(2,1)S(1)}, u32[]{:S(2)}, u32[]{:S(2)}) %all-to-all-start.1) | async-done | bytes 2621472 | tf_op jit(solution)/shard_map/all_to_all | solution.py:20
  148.3 3.7 reshape.57
  152.1 3.5 copy.33
  155.6 0.6 convert_reduce_fusion
  156.2 0.0 copy-start.14
  156.2 0.0 copy-start.17
  156.2 0.0 copy-start.18
  156.2 0.0 copy-start.13
  156.2 0.0 copy-start.15
  156.2 0.0 copy-start.16
  156.2 0.5 fusion.3
  156.8 6.2 %all-reduce.2 = (f32[512]{0:T(512)S(1)}, f32[640]{0:T(1024)S(1)}, f32[512]{0:T(512)S(1)}) all-reduce(f32[512]{0:T(512)S(1)} %get-tuple-element.17, f32[640]{0:T(1024)S(1)} %get-tuple-element.15, f32[512]{0:T(512)S(1)} %get-tuple-element.19), channel_id=1, replica_groups=mesh['dp'=2,'row'=4,'col'=4] {'col'}, use_global_device_ids=true, to_apply=%region_2.0 | all-reduce | flops 1664 | bytes 13312 | tf_op jit(solution)/shard_map/psum | solution.py:57
  163.0 0.6 fusion.10
  163.6 0.6 fusion.9
  164.2 38.0 %all-reduce.1 = (f32[1280]{0:T(1024)S(1)}, f32[]{:T(128)}, f32[1024]{0:T(1024)S(1)}, f32[]{:T(128)}, f32[1024]{0:T(1024)S(1)}, /*index=5*/f32[]{:T(128)}) all-reduce(f32[1280]{0:T(1024)S(1)} %get-tuple-element.18, f32[]{:T(128)} %get-tuple-element.48, ...), channel_id=1, replica_groups=mesh['dp'=2,'row'=4,'col'=4] {'dp','row'}, use_global_device_ids=true, to_apply=%region_6.0 | all-reduce | flops 3331 | bytes 26648 | tf_op jit(solution)/shard_map/psum | solution.py:59
  203.5 0.0 copy-start.7
  203.5 0.0 copy-start.10
  204.2 0.0 copy-start.8
  204.2 0.0 copy-start.2
  204.2 3.8 multiply_reduce_fusion.1
  208.0 2.3 multiply_reduce_fusion
  210.3 2.0 multiply_reduce_fusion.2
  212.2 37.2 %all-reduce = (f32[]{:T(128)}, f32[]{:T(128)}, f32[]{:T(128)}) all-reduce(f32[]{:T(128)} %multiply_reduce_fusion.1, f32[]{:T(128)} %multiply_reduce_fusion, f32[]{:T(128)} %multiply_reduce_fusion.2), channel_id=1, replica_groups=mesh['dp'=2,'row'=4,'col'=4] {'dp','row','col'}, use_global_device_ids=true, to_apply=%region_8.0 | all-reduce | flops 3 | bytes 24 | tf_op jit(solution)/shard_map/psum | solution.py:67
  250.2 5.9 %fusion.6 = (bf16[512,1024]{1,0:T(8,128)(2,1)}, f32[512,1024]{1,0:T(8,128)}, f32[512,1024]{1,0:T(8,128)}) fusion(f32[512,1024]{1,0:T(8,128)} %param.21, f32[]{:T(128)S(6)} %max.11, f32[1024]{0:T(1024)S(1)} %multiply_add_fusion.4, f32[512]{0:T(512)S(1)} %get-tuple-element.77, f32[]{:T(128)S(6)} %div.136, f32[512,1024]{1,0:T(8,128)} %copy-done.1), kind=kLoop, calls=%fused_computation.30 | loop fusion | flops 4194304 | bytes 9443336 | tf_op jit(solution)/shard_map/convert_element_type | solution.py:15
  256.1 0.0 all-gather.8.cloned.1.call-update
  256.1 0.0 all-gather.4.cloned.1.call-start
  256.9 6.7 %fusion.8 = (bf16[512,1280]{1,0:T(8,128)(2,1)}, f32[512,1280]{1,0:T(8,128)}, f32[512,1280]{1,0:T(8,128)}) fusion(f32[512,1280]{1,0:T(8,128)} %param.13, f32[]{:T(128)S(6)} %max.9, f32[1280]{0:T(1024)S(1)} %multiply_add_fusion.3, f32[512]{0:T(512)S(1)} %get-tuple-element.67, f32[]{:T(128)S(6)} %div.112, f32[512,1280]{1,0:T(8,128)} %copy-done), kind=kLoop, calls=%fused_computation.32 | loop fusion | flops 5242880 | bytes 11803656 | tf_op jit(solution)/shard_map/convert_element_type | solution.py:15
  263.5 0.0 all-gather.4.cloned.1.call-update
  263.5 0.0 all-gather.6.cloned.1.call-start
  264.3 6.3 %fusion.7 = (bf16[640,1024]{1,0:T(8,128)(2,1)}, f32[640,1024]{1,0:T(8,128)}, f32[640,1024]{1,0:T(8,128)}) fusion(f32[640,1024]{1,0:T(8,128)} %param.17, f32[]{:T(128)S(6)} %max.10, f32[1024]{0:T(1024)S(1)} %multiply_add_fusion.5, f32[640]{0:T(1024)S(1)} %get-tuple-element.72, f32[]{:T(128)S(6)} %div.124, f32[640,1024]{1,0:T(8,128)S(1)} %convert_reduce_fusion), kind=kLoop, calls=%fused_computation.31 | loop fusion | flops 5242880 | bytes 11803144 | tf_op jit(solution)/shard_map/convert_element_type | solution.py:15
  270.5 0.0 all-gather.6.cloned.1.call-update
  270.6 20.2 %all-gather.8.cloned.1.call-done = bf16[1024,1024]{1,0:T(8,128)(2,1)} async-done(((bf16[512,1024]{1,0:T(8,128)(2,1)}), bf16[1024,1024]{1,0:T(8,128)(2,1)}) %all-gather.8.cloned.1.call-update) | async-done | bytes 2097168 | tf_op jit(solution)/shard_map/all_gather | solution.py:15
  290.7 41.1 %all-gather.4.cloned.1.call-done = bf16[1024,1280]{1,0:T(8,128)(2,1)} async-done(((bf16[512,1280]{1,0:T(8,128)(2,1)}), bf16[1024,1280]{1,0:T(8,128)(2,1)}) %all-gather.4.cloned.1.call-update) | async-done | bytes 2621456 | tf_op jit(solution)/shard_map/all_gather | solution.py:15
  331.9 41.2 %all-gather.6.cloned.1.call-done = bf16[1280,1024]{1,0:T(8,128)(2,1)} async-done(((bf16[640,1024]{1,0:T(8,128)(2,1)}), bf16[1280,1024]{1,0:T(8,128)(2,1)}) %all-gather.6.cloned.1.call-update) | async-done | bytes 2621456 | tf_op jit(solution)/shard_map/all_gather | solution.py:15
  373.1 3.5 copy.45
  376.6 1.5 copy.46
  378.1 1.0 copy-done.6
  379.1 1.3 copy.47
  (28 shorter events, 0.1 us)
Async XLA Ops:
  29.7 5.5 %copy-start.4 = (bf16[1,1024,1280]{2,1,0:T(8,128)(2,1)S(1)}, bf16[1,1024,1280]{2,1,0:T(8,128)(2,1)}, u32[]{:S(2)}) copy-start(bf16[1,1024,1280]{2,1,0:T(8,128)(2,1)} %param.12) | copy-start | bytes 7864324
  29.7 40.3 %all-to-all-start.2 = ((bf16[2,2,262144]{2,1,0:T(2,128)(2,1)}), bf16[2,2,262144]{2,1,0:T(2,128)(2,1)}, u32[]{:S(2)}, u32[]{:S(2)}) async-start(bf16[2,2,262144]{2,1,0:T(2,128)(2,1)} %reshape.58), calls=%async_computation.2 | async-start | bytes 4194304 | tf_op jit(solution)/shard_map/all_to_all | solution.py:20
  70.0 5.8 %copy-start.5 = (bf16[1,1280,1024]{2,1,0:T(8,128)(2,1)S(1)}, bf16[1,1280,1024]{2,1,0:T(8,128)(2,1)}, u32[]{:S(2)}) copy-start(bf16[1,1280,1024]{2,1,0:T(8,128)(2,1)} %param.16) | copy-start | bytes 7864324
  70.0 42.6 %all-to-all-start = ((bf16[2,2,327680]{2,1,0:T(2,128)(2,1)}), bf16[2,2,327680]{2,1,0:T(2,128)(2,1)}, u32[]{:S(2)}, u32[]{:S(2)}) async-start(bf16[2,2,327680]{2,1,0:T(2,128)(2,1)} %reshape.54), calls=%async_computation | async-start | bytes 5242880 | tf_op jit(solution)/shard_map/all_to_all | solution.py:20
  112.6 35.7 %all-to-all-start.1 = ((bf16[2,2,327680]{2,1,0:T(2,128)(2,1)}), bf16[2,2,327680]{2,1,0:T(2,128)(2,1)S(1)}, u32[]{:S(2)}, u32[]{:S(2)}) async-start(bf16[2,2,327680]{2,1,0:T(2,128)(2,1)} %reshape.56), calls=%async_computation.1 | async-start | bytes 5242880 | tf_op jit(solution)/shard_map/all_to_all | solution.py:20
  116.8 174.0 %all-gather.8.cloned.1.call-start = ((), (), s32[]{:S(2)}) async-start(), calls=%async_computation.5 | async-start | bytes 3145728 | tf_op jit(solution)/shard_map/all_gather | solution.py:15
  124.7 1.3 copy-start.1
  134.9 1.5 copy-start
  156.2 6.8 %copy-start.14 = (f32[640]{0:T(1024)S(1)}, f32[640]{0:T(1024)}, u32[]{:S(2)}) copy-start(f32[640]{0:T(1024)} %param.18) | copy-start | bytes 7684
  156.2 7.4 %copy-start.17 = (f32[512]{0:T(512)S(1)}, f32[512]{0:T(512)}, u32[]{:S(2)}) copy-start(f32[512]{0:T(512)} %param.22) | copy-start | bytes 6148
  156.2 7.4 %copy-start.18 = (f32[512]{0:T(512)S(1)}, f32[512]{0:T(512)}, u32[]{:S(2)}) copy-start(f32[512]{0:T(512)} %param.14) | copy-start | bytes 6148
  156.2 47.3 %copy-start.13 = (f32[1280]{0:T(1024)S(1)}, f32[1280]{0:T(1024)}, u32[]{:S(2)}) copy-start(f32[1280]{0:T(1024)} %param.15) | copy-start | bytes 15364
  156.2 47.3 %copy-start.15 = (f32[1024]{0:T(1024)S(1)}, f32[1024]{0:T(1024)}, u32[]{:S(2)}) copy-start(f32[1024]{0:T(1024)} %param.19) | copy-start | bytes 12292
  156.2 48.0 %copy-start.16 = (f32[1024]{0:T(1024)S(1)}, f32[1024]{0:T(1024)}, u32[]{:S(2)}) copy-start(f32[1024]{0:T(1024)} %param.23) | copy-start | bytes 12292
  163.6 100.7 %copy-start.9 = (f32[640]{0:T(1024)}, f32[640]{0:T(1024)S(1)}, u32[]{:S(2)}) copy-start(f32[640]{0:T(1024)S(1)} %get-tuple-element.72) | copy-start | bytes 7684
  164.2 86.0 %copy-start.11 = (f32[512]{0:T(512)}, f32[512]{0:T(512)S(1)}, u32[]{:S(2)}) copy-start(f32[512]{0:T(512)S(1)} %get-tuple-element.77) | copy-start | bytes 6148
  164.2 92.6 %copy-start.12 = (f32[512]{0:T(512)}, f32[512]{0:T(512)S(1)}, u32[]{:S(2)}) copy-start(f32[512]{0:T(512)S(1)} %get-tuple-element.67) | copy-start | bytes 6148
  203.5 53.3 %copy-start.7 = (f32[1280]{0:T(1024)}, f32[1280]{0:T(1024)S(1)}, u32[]{:S(2)}) copy-start(f32[1280]{0:T(1024)S(1)} %multiply_add_fusion.3) | copy-start | bytes 15364
  203.5 60.7 %copy-start.10 = (f32[1024]{0:T(1024)}, f32[1024]{0:T(1024)S(1)}, u32[]{:S(2)}) copy-start(f32[1024]{0:T(1024)S(1)} %multiply_add_fusion.5) | copy-start | bytes 12292
  204.2 46.0 %copy-start.8 = (f32[1024]{0:T(1024)}, f32[1024]{0:T(1024)S(1)}, u32[]{:S(2)}) copy-start(f32[1024]{0:T(1024)S(1)} %multiply_add_fusion.4) | copy-start | bytes 12292
  204.2 6.1 %copy-start.2 = (f32[512,1024]{1,0:T(8,128)S(1)}, f32[512,1024]{1,0:T(8,128)}, u32[]{:S(2)}) copy-start(f32[512,1024]{1,0:T(8,128)} %copy-done.1) | copy-start | bytes 6291460
  256.1 75.8 %all-gather.4.cloned.1.call-start = ((), (), s32[]{:S(2)}) async-start(), calls=%async_computation.3 | async-start | bytes 3932160 | tf_op jit(solution)/shard_map/all_gather | solution.py:15
  263.5 109.5 %all-gather.6.cloned.1.call-start = ((), (), s32[]{:S(2)}) async-start(), calls=%async_computation.4 | async-start | bytes 3932160 | tf_op jit(solution)/shard_map/all_gather | solution.py:15
  373.1 3.6 copy-start.3
  376.6 2.5 copy-start.6
Sparse Core Ops, SparseCore 0:
  256.2 34.4 all-gather.7
  292.9 38.9 all-gather.3
  334.0 38.9 all-gather.5
where the time goes:
time: 393 us; the launch traced here: 387 us
  waiting for transfers between devices  114 us (29%)
  other arithmetic  86.1 us (22%)
  blocking collectives  81.4 us (21%)
  local copies, waits for them, and re-layouts  71.9 us (18%)
  between operations  18.3 us (5%)
  starting transfers between devices  15.7 us (4%)
    all_gather x3, waiting for transfers between devices, finish(): lax.all_gather(updated.astype(jnp.bfloat16), 'dp', axis=0, tiled=True)  102 us
    unnamed x51, local copies, waits for them, and re-layouts  62.5 us
    unnamed x3, other arithmetic  55 us
    psum x1, blocking collectives, body(): lax.psum((column_parts[which], jnp.sum(rows_next)), ('dp', 'row'))  38 us
    psum x1, blocking collectives, body(): lax.psum(jnp.sum(update_raw * update_raw), ('dp', 'row', 'col'))  37.2 us
    convert_element_type x3, other arithmetic, finish(): updated.astype(jnp.bfloat16)  18.8 us
    all_to_all x3, starting transfers between devices, reduce_gradient(): lax.all_to_all(gradient, 'dp', split_axis=1, concat_axis=0, tiled=True)  15.4 us
    all_to_all x3, waiting for transfers between devices, reduce_gradient(): lax.all_to_all(gradient, 'dp', split_axis=1, concat_axis=0, tiled=True)  11.3 us
  transfers between devices with their start and end apart: 6, of which 4 were waited for; matrix products, arithmetic and copies ran while one was open for 26% of the time, Pallas kernels for 0%

commit v1 on v0

--- a/solution.py
+++ b/solution.py
@@ -17,7 +17,9 @@
 
 
 def reduce_gradient(gradient, dp_count):
-    received = lax.all_to_all(gradient, "dp", split_axis=1, concat_axis=0, tiled=True)
+    received = jnp.concatenate(
+        lax.all_to_all(jnp.stack(jnp.split(gradient, lax.axis_size("dp"), axis=1)), "dp", 0, 0), 0
+    )
     summed = jnp.sum(received.astype(jnp.float32), axis=0)
     return summed / dp_count
 

time: 393 us -> 345 us (0.88); the launches traced: 387 us -> 344 us
  waiting for transfers between devices: 114 us -> 174 us
  local copies, waits for them, and re-layouts: 71.9 us -> 18.1 us
  other arithmetic: 86.1 us -> 40.1 us
    all_to_all x3, waiting for transfers between devices: 11.3 us -> 71.9 us  [reduce_gradient(): lax.all_to_all(jnp.stack(jnp.split(gradient, lax.axis_size('dp'), axis=1)...]
    unnamed x3 -> x0, other arithmetic: 55 us -> none
    unnamed x51 -> x43, local copies, waits for them, and re-layouts: 62.5 us -> 12.5 us
    all_to_all x3 -> x0, local copies, waits for them, and re-layouts: 9.41 us -> none  [reduce_gradient(): lax.all_to_all(gradient, 'dp', split_axis=1, concat_axis=0, tiled=True)]
    another operation x0 -> x3, local copies, waits for them, and re-layouts: none -> 5.54 us  [reduce_gradient(): jnp.stack(jnp.split(gradient, lax.axis_size('dp'), axis=1))]
    another operation x0 -> x3, other arithmetic: none -> 4.94 us  [reduce_gradient(): jnp.stack(jnp.split(gradient, lax.axis_size('dp'), axis=1))]
    reduce_sum x3, other arithmetic: 1.47 us -> 5.43 us  [reduce_gradient(): summed = jnp.sum(received.astype(jnp.float32), axis=0)]
  transfers between devices with their start and end apart: 6 -> 6, of which waited for: 4 -> 6; matrix products, arithmetic and copies ran while one was open for 26% -> 7% of each run, Pallas kernels for 0% -> 0%
where the time goes in v1:
time: 345 us; the launch traced here: 344 us
  waiting for transfers between devices  174 us (50%)
  blocking collectives  80.5 us (23%)
  other arithmetic  40.1 us (12%)
  local copies, waits for them, and re-layouts  18.1 us (5%)
  between operations  18 us (5%)
  starting transfers between devices  13.2 us (4%)
    all_gather x3, waiting for transfers between devices, finish(): lax.all_gather(updated.astype(jnp.bfloat16), 'dp', axis=0, tiled=True)  102 us
    all_to_all x3, waiting for transfers between devices, reduce_gradient(): lax.all_to_all(jnp.stack(jnp.split(gradient, lax.axis_size('dp'), axis=1)...  71.9 us
    psum x1, blocking collectives, body(): lax.psum(jnp.sum(update_raw * update_raw), ('dp', 'row', 'col'))  37.6 us
    psum x1, blocking collectives, body(): lax.psum((column_parts[which], jnp.sum(rows_next)), ('dp', 'row'))  37.2 us
    convert_element_type x3, other arithmetic, finish(): updated.astype(jnp.bfloat16)  19 us
    all_to_all x3, starting transfers between devices, reduce_gradient(): lax.all_to_all(jnp.stack(jnp.split(gradient, lax.axis_size('dp'), axis=1)...  13.1 us
    unnamed x43, local copies, waits for them, and re-layouts  12.5 us
    reduce_sum x3, other arithmetic, body(): jnp.sum(update_raw * update_raw)  8 us
  transfers between devices with their start and end apart: 6, of which 6 were waited for; matrix products, arithmetic and copies ran while one was open for 7% of the time, Pallas kernels for 0%

profile of v1, /device:TPU:0, one launch (start us, length us, event | category | flops | bytes accessed | tf_op | source)
XLA Modules:
  0.0 344.4 jit_solution(3970008219703649295)
XLA Ops:
  7.2 1.7 slice_bitcast_fusion.5
  8.9 1.5 pad_maximum_fusion.2
  10.4 4.2 %all-to-all-start.2 = ((bf16[2,1,512,1024]{3,2,1,0:T(8,128)(2,1)}), bf16[2,1,512,1024]{3,2,1,0:T(8,128)(2,1)S(1)}, u32[]{:S(2)}, u32[]{:S(2)}) async-start(bf16[2,1,512,1024]{3,2,1,0:T(8,128)(2,1)} %pad_maximum_fusion.2), calls=%async_computation.2 | async-start | bytes 4194304 | tf_op jit(solution)/shard_map/all_to_all | solution.py:21
  14.6 1.9 slice_bitcast_fusion.3
  16.5 1.7 pad_maximum_fusion
  18.2 22.3 %all-to-all-done.2 = bf16[2,1,512,1024]{3,2,1,0:T(8,128)(2,1)S(1)} async-done(((bf16[2,1,512,1024]{3,2,1,0:T(8,128)(2,1)}), bf16[2,1,512,1024]{3,2,1,0:T(8,128)(2,1)S(1)}, u32[]{:S(2)}, u32[]{:S(2)}) %all-to-all-start.2) | async-done | bytes 2097184 | tf_op jit(solution)/shard_map/all_to_all | solution.py:21
  40.5 1.3 copy-done.5
  41.8 3.9 %all-to-all-start = ((bf16[2,1,512,1280]{3,2,1,0:T(8,128)(2,1)}), bf16[2,1,512,1280]{3,2,1,0:T(8,128)(2,1)S(1)}, u32[]{:S(2)}, u32[]{:S(2)}) async-start(bf16[2,1,512,1280]{3,2,1,0:T(8,128)(2,1)} %pad_maximum_fusion), calls=%async_computation | async-start | bytes 5242880 | tf_op jit(solution)/shard_map/all_to_all | solution.py:21
  45.7 2.0 slice_bitcast_fusion.1
  47.6 1.7 pad_maximum_fusion.1
  49.3 26.5 %all-to-all-done = bf16[2,1,512,1280]{3,2,1,0:T(8,128)(2,1)S(1)} async-done(((bf16[2,1,512,1280]{3,2,1,0:T(8,128)(2,1)}), bf16[2,1,512,1280]{3,2,1,0:T(8,128)(2,1)S(1)}, u32[]{:S(2)}, u32[]{:S(2)}) %all-to-all-start) | async-done | bytes 2621472 | tf_op jit(solution)/shard_map/all_to_all | solution.py:21
  75.8 1.5 copy-done.3
  77.3 5.0 %all-to-all-start.1 = ((bf16[2,1,640,1024]{3,2,1,0:T(8,128)(2,1)}), bf16[2,1,640,1024]{3,2,1,0:T(8,128)(2,1)}, u32[]{:S(2)}, u32[]{:S(2)}) async-start(bf16[2,1,640,1024]{3,2,1,0:T(8,128)(2,1)} %pad_maximum_fusion.1), calls=%async_computation.1 | async-start | bytes 5242880 | tf_op jit(solution)/shard_map/all_to_all | solution.py:21
  82.3 0.0 all-gather.8.cloned.1.call-start
  82.4 0.0 copy-start.4
  82.4 2.4 convert_reduce_fusion.2
  84.8 0.0 copy-start.1
  84.8 1.3 copy-done.1
  86.1 0.5 fusion.5
  86.6 0.0 copy-done.4
  86.6 0.5 convert_reduce_fusion.1
  87.0 0.0 copy-start
  87.0 0.6 fusion.1
  87.6 0.9 copy-done
  88.5 23.2 %all-to-all-done.1 = bf16[2,1,640,1024]{3,2,1,0:T(8,128)(2,1)} async-done(((bf16[2,1,640,1024]{3,2,1,0:T(8,128)(2,1)}), bf16[2,1,640,1024]{3,2,1,0:T(8,128)(2,1)}, u32[]{:S(2)}, u32[]{:S(2)}) %all-to-all-start.1) | async-done | bytes 2621472 | tf_op jit(solution)/shard_map/all_to_all | solution.py:21
  111.7 2.6 convert_reduce_fusion
  114.3 0.0 copy-start.15
  114.3 0.0 copy-start.18
  114.3 0.0 copy-start.19
  114.3 0.0 copy-start.14
  114.3 0.0 copy-start.16
  114.3 0.0 copy-start.17
  114.3 0.5 fusion.3
  114.9 5.8 %all-reduce.2 = (f32[512]{0:T(512)S(1)}, f32[640]{0:T(1024)S(1)}, f32[512]{0:T(512)S(1)}) all-reduce(f32[512]{0:T(512)S(1)} %get-tuple-element.17, f32[640]{0:T(1024)S(1)} %get-tuple-element.15, f32[512]{0:T(512)S(1)} %get-tuple-element.19), channel_id=1, replica_groups=mesh['dp'=2,'row'=4,'col'=4] {'col'}, use_global_device_ids=true, to_apply=%region_2.0 | all-reduce | flops 1664 | bytes 13312 | tf_op jit(solution)/shard_map/psum | solution.py:59
  120.6 0.0 copy-done.15
  120.6 0.6 fusion.10
  121.2 0.0 copy-done.18
  121.3 0.0 copy-done.19
  121.3 0.6 fusion.9
  121.9 37.2 %all-reduce.1 = (f32[1280]{0:T(1024)S(1)}, f32[]{:T(128)}, f32[1024]{0:T(1024)S(1)}, f32[]{:T(128)}, f32[1024]{0:T(1024)S(1)}, /*index=5*/f32[]{:T(128)}) all-reduce(f32[1280]{0:T(1024)S(1)} %get-tuple-element.18, f32[]{:T(128)} %get-tuple-element.54, ...), channel_id=1, replica_groups=mesh['dp'=2,'row'=4,'col'=4] {'dp','row'}, use_global_device_ids=true, to_apply=%region_6.0 | all-reduce | flops 3331 | bytes 26648 | tf_op jit(solution)/shard_map/psum | solution.py:61
  160.3 0.0 copy-done.14
  160.4 0.0 copy-start.8
  160.4 0.0 copy-start.11
  161.1 0.0 copy-start.9
  161.1 0.0 copy-start.2
  161.1 3.8 %multiply_reduce_fusion.1 = f32[]{:T(128)} fusion(f32[1280]{0:T(1024)S(1)} %multiply_add_fusion.3, f32[512]{0:T(512)S(1)} %get-tuple-element.73, f32[]{:T(128)S(6)} %div.112, f32[512,1280]{1,0:T(8,128)} %copy-done), kind=kLoop, calls=%fused_computation.10 | loop fusion | flops 3932159 | bytes 2628616 | tf_op jit(solution)/shard_map/reduce_sum | solution.py:69
  164.9 2.3 multiply_reduce_fusion
  167.2 2.0 multiply_reduce_fusion.2
  169.1 37.6 %all-reduce = (f32[]{:T(128)}, f32[]{:T(128)}, f32[]{:T(128)}) all-reduce(f32[]{:T(128)} %multiply_reduce_fusion.1, f32[]{:T(128)} %multiply_reduce_fusion, f32[]{:T(128)} %multiply_reduce_fusion.2), channel_id=1, replica_groups=mesh['dp'=2,'row'=4,'col'=4] {'dp','row','col'}, use_global_device_ids=true, to_apply=%region_8.0 | all-reduce | flops 3 | bytes 24 | tf_op jit(solution)/shard_map/psum | solution.py:69
  207.4 5.9 %fusion.6 = (bf16[512,1024]{1,0:T(8,128)(2,1)}, f32[512,1024]{1,0:T(8,128)}, f32[512,1024]{1,0:T(8,128)}) fusion(f32[512,1024]{1,0:T(8,128)} %param.21, f32[]{:T(128)S(6)} %max.11, f32[1024]{0:T(1024)S(1)} %multiply_add_fusion.4, f32[512]{0:T(512)S(1)} %get-tuple-element.83, f32[]{:T(128)S(6)} %div.136, f32[512,1024]{1,0:T(8,128)} %copy-done.1), kind=kLoop, calls=%fused_computation.39 | loop fusion | flops 4194304 | bytes 9443336 | tf_op jit(solution)/shard_map/convert_element_type | solution.py:15
  213.3 0.0 all-gather.8.cloned.1.call-update
  213.3 0.0 all-gather.4.cloned.1.call-start
  214.1 6.7 %fusion.8 = (bf16[512,1280]{1,0:T(8,128)(2,1)}, f32[512,1280]{1,0:T(8,128)}, f32[512,1280]{1,0:T(8,128)}) fusion(f32[512,1280]{1,0:T(8,128)} %param.13, f32[]{:T(128)S(6)} %max.9, f32[1280]{0:T(1024)S(1)} %multiply_add_fusion.3, f32[512]{0:T(512)S(1)} %get-tuple-element.73, f32[]{:T(128)S(6)} %div.112, f32[512,1280]{1,0:T(8,128)} %copy-done), kind=kLoop, calls=%fused_computation.41 | loop fusion | flops 5242880 | bytes 11803656 | tf_op jit(solution)/shard_map/convert_element_type | solution.py:15
  220.8 0.0 all-gather.4.cloned.1.call-update
  220.8 0.0 all-gather.6.cloned.1.call-start
  221.5 6.4 %fusion.7 = (bf16[640,1024]{1,0:T(8,128)(2,1)}, f32[640,1024]{1,0:T(8,128)}, f32[640,1024]{1,0:T(8,128)}) fusion(f32[640,1024]{1,0:T(8,128)} %param.17, f32[]{:T(128)S(6)} %max.10, f32[1024]{0:T(1024)S(1)} %multiply_add_fusion.5, f32[640]{0:T(1024)S(1)} %get-tuple-element.78, f32[]{:T(128)S(6)} %div.124, f32[640,1024]{1,0:T(8,128)S(1)} %convert_reduce_fusion), kind=kLoop, calls=%fused_computation.40 | loop fusion | flops 5242880 | bytes 11803144 | tf_op jit(solution)/shard_map/convert_element_type | solution.py:15
  227.9 0.0 all-gather.6.cloned.1.call-update
  227.9 20.2 %all-gather.8.cloned.1.call-done = bf16[1024,1024]{1,0:T(8,128)(2,1)} async-done(((bf16[512,1024]{1,0:T(8,128)(2,1)}), bf16[1024,1024]{1,0:T(8,128)(2,1)}) %all-gather.8.cloned.1.call-update) | async-done | bytes 2097168 | tf_op jit(solution)/shard_map/all_gather | solution.py:15
  248.1 41.1 %all-gather.4.cloned.1.call-done = bf16[1024,1280]{1,0:T(8,128)(2,1)} async-done(((bf16[512,1280]{1,0:T(8,128)(2,1)}), bf16[1024,1280]{1,0:T(8,128)(2,1)}) %all-gather.4.cloned.1.call-update) | async-done | bytes 2621456 | tf_op jit(solution)/shard_map/all_gather | solution.py:15
  289.3 41.2 %all-gather.6.cloned.1.call-done = bf16[1280,1024]{1,0:T(8,128)(2,1)} async-done(((bf16[640,1024]{1,0:T(8,128)(2,1)}), bf16[1280,1024]{1,0:T(8,128)(2,1)}) %all-gather.6.cloned.1.call-update) | async-done | bytes 2621456 | tf_op jit(solution)/shard_map/all_gather | solution.py:15
  330.4 3.5 %copy.30 = bf16[1024,1280]{1,0:T(8,128)(2,1)} copy(bf16[1024,1280]{1,0:T(8,128)(2,1)} %all-gather.4.cloned.1.call-done) | data formatting | bytes 5242880
  334.0 1.5 copy.31
  335.5 1.0 copy-done.7
  336.5 1.3 copy.32
  (20 shorter events, 0.0 us)
Async XLA Ops:
  10.4 30.1 %all-to-all-start.2 = ((bf16[2,1,512,1024]{3,2,1,0:T(8,128)(2,1)}), bf16[2,1,512,1024]{3,2,1,0:T(8,128)(2,1)S(1)}, u32[]{:S(2)}, u32[]{:S(2)}) async-start(bf16[2,1,512,1024]{3,2,1,0:T(8,128)(2,1)} %pad_maximum_fusion.2), calls=%async_computation.2 | async-start | bytes 4194304 | tf_op jit(solution)/shard_map/all_to_all | solution.py:21
  40.5 1.3 copy-start.5
  41.8 34.0 %all-to-all-start = ((bf16[2,1,512,1280]{3,2,1,0:T(8,128)(2,1)}), bf16[2,1,512,1280]{3,2,1,0:T(8,128)(2,1)S(1)}, u32[]{:S(2)}, u32[]{:S(2)}) async-start(bf16[2,1,512,1280]{3,2,1,0:T(8,128)(2,1)} %pad_maximum_fusion), calls=%async_computation | async-start | bytes 5242880 | tf_op jit(solution)/shard_map/all_to_all | solution.py:21
  75.8 1.5 copy-start.3
  77.3 34.4 %all-to-all-start.1 = ((bf16[2,1,640,1024]{3,2,1,0:T(8,128)(2,1)}), bf16[2,1,640,1024]{3,2,1,0:T(8,128)(2,1)}, u32[]{:S(2)}, u32[]{:S(2)}) async-start(bf16[2,1,640,1024]{3,2,1,0:T(8,128)(2,1)} %pad_maximum_fusion.1), calls=%async_computation.1 | async-start | bytes 5242880 | tf_op jit(solution)/shard_map/all_to_all | solution.py:21
  82.3 165.8 %all-gather.8.cloned.1.call-start = ((), (), s32[]{:S(2)}) async-start(), calls=%async_computation.5 | async-start | bytes 3145728 | tf_op jit(solution)/shard_map/all_gather | solution.py:15
  82.4 4.2 %copy-start.4 = (bf16[2,1,512,1280]{3,2,1,0:T(8,128)(2,1)S(1)}, bf16[2,1,512,1280]{3,2,1,0:T(8,128)(2,1)}, u32[]{:S(2)}) copy-start(bf16[2,1,512,1280]{3,2,1,0:T(8,128)(2,1)} %copy-done.3) | copy-start | bytes 7864324
  84.8 1.3 copy-start.1
  87.0 1.5 copy-start
  114.3 6.4 %copy-start.15 = (f32[640]{0:T(1024)S(1)}, f32[640]{0:T(1024)}, u32[]{:S(2)}) copy-start(f32[640]{0:T(1024)} %param.18) | copy-start | bytes 7684
  114.3 7.0 %copy-start.18 = (f32[512]{0:T(512)S(1)}, f32[512]{0:T(512)}, u32[]{:S(2)}) copy-start(f32[512]{0:T(512)} %param.22) | copy-start | bytes 6148
  114.3 7.0 %copy-start.19 = (f32[512]{0:T(512)S(1)}, f32[512]{0:T(512)}, u32[]{:S(2)}) copy-start(f32[512]{0:T(512)} %param.14) | copy-start | bytes 6148
  114.3 46.0 %copy-start.14 = (f32[1280]{0:T(1024)S(1)}, f32[1280]{0:T(1024)}, u32[]{:S(2)}) copy-start(f32[1280]{0:T(1024)} %param.15) | copy-start | bytes 15364
  114.3 46.1 %copy-start.16 = (f32[1024]{0:T(1024)S(1)}, f32[1024]{0:T(1024)}, u32[]{:S(2)}) copy-start(f32[1024]{0:T(1024)} %param.19) | copy-start | bytes 12292
  114.3 46.7 %copy-start.17 = (f32[1024]{0:T(1024)S(1)}, f32[1024]{0:T(1024)}, u32[]{:S(2)}) copy-start(f32[1024]{0:T(1024)} %param.23) | copy-start | bytes 12292
  121.2 100.2 %copy-start.10 = (f32[640]{0:T(1024)}, f32[640]{0:T(1024)S(1)}, u32[]{:S(2)}) copy-start(f32[640]{0:T(1024)S(1)} %get-tuple-element.78) | copy-start | bytes 7684
  121.9 85.5 %copy-start.12 = (f32[512]{0:T(512)}, f32[512]{0:T(512)S(1)}, u32[]{:S(2)}) copy-start(f32[512]{0:T(512)S(1)} %get-tuple-element.83) | copy-start | bytes 6148
  121.9 92.2 %copy-start.13 = (f32[512]{0:T(512)}, f32[512]{0:T(512)S(1)}, u32[]{:S(2)}) copy-start(f32[512]{0:T(512)S(1)} %get-tuple-element.73) | copy-start | bytes 6148
  160.4 53.7 %copy-start.8 = (f32[1280]{0:T(1024)}, f32[1280]{0:T(1024)S(1)}, u32[]{:S(2)}) copy-start(f32[1280]{0:T(1024)S(1)} %multiply_add_fusion.3) | copy-start | bytes 15364
  160.4 61.1 %copy-start.11 = (f32[1024]{0:T(1024)}, f32[1024]{0:T(1024)S(1)}, u32[]{:S(2)}) copy-start(f32[1024]{0:T(1024)S(1)} %multiply_add_fusion.5) | copy-start | bytes 12292
  161.1 46.3 %copy-start.9 = (f32[1024]{0:T(1024)}, f32[1024]{0:T(1024)S(1)}, u32[]{:S(2)}) copy-start(f32[1024]{0:T(1024)S(1)} %multiply_add_fusion.4) | copy-start | bytes 12292
  161.1 6.1 %copy-start.2 = (f32[512,1024]{1,0:T(8,128)S(1)}, f32[512,1024]{1,0:T(8,128)}, u32[]{:S(2)}) copy-start(f32[512,1024]{1,0:T(8,128)} %copy-done.1) | copy-start | bytes 6291460
  213.3 75.9 %all-gather.4.cloned.1.call-start = ((), (), s32[]{:S(2)}) async-start(), calls=%async_computation.3 | async-start | bytes 3932160 | tf_op jit(solution)/shard_map/all_gather | solution.py:15
  220.8 109.6 %all-gather.6.cloned.1.call-start = ((), (), s32[]{:S(2)}) async-start(), calls=%async_computation.4 | async-start | bytes 3932160 | tf_op jit(solution)/shard_map/all_gather | solution.py:15
  330.4 3.6 %copy-start.6 = (bf16[1280,1024]{1,0:T(8,128)(2,1)S(1)}, bf16[1280,1024]{1,0:T(8,128)(2,1)}, u32[]{:S(2)}) copy-start(bf16[1280,1024]{1,0:T(8,128)(2,1)} %all-gather.6.cloned.1.call-done) | copy-start | bytes 7864324
  334.0 2.5 copy-start.7
Sparse Core Ops, SparseCore 0:
  213.5 34.6 all-gather.7
  250.2 38.9 all-gather.3
  291.4 38.9 all-gather.5
